TPU v7x, 32 devices: a whole 2x2x4 slice. The times are simulated.
32 devices in a mesh: dp: 8 (over z, x), tensor: 4 (over y, core).
Axes of the slice: x: 2, y: 2, z: 4, core: 2. Of those that a mesh axis runs over, the one named last changes fastest.
Arguments:
- tokens: bfloat16 [20480, 768], P(('dp', 'tensor')), may hold values from -6 to 6
- cotangent: bfloat16 [20480, 768], P(('dp', 'tensor')), may hold values from -6 to 6
- lengths: int32 [8, 8], P('dp'), may hold values from 1 to 512, 2048 in all within a row
- w_qkv: bfloat16 [768, 3, 768], P('dp', None, 'tensor'), may hold values from -0.21875 to 0.21875
- w_out: bfloat16 [768, 768], P('tensor', 'dp'), may hold values from -6 to 6
- w_fc: bfloat16 [768, 3072], P('dp', 'tensor'), may hold values from -0.21875 to 0.21875
- w_proj: bfloat16 [3072, 768], P('tensor', 'dp'), may hold values from -0.109375 to 0.109375
- ln1_gain: bfloat16 [768], P('dp'), may hold values from 0.25 to 1.75
- ln1_bias: bfloat16 [768], P('dp'), may hold values from -3 to 3
- ln2_gain: bfloat16 [768], P('dp'), may hold values from 0.25 to 1.75
- ln2_bias: bfloat16 [768], P('dp'), may hold values from -3 to 3
Outputs:
- block_out: bfloat16 [20480, 768], P(('dp', 'tensor'))
- input_grad: bfloat16 [20480, 768], P(('dp', 'tensor'))
- w_qkv_grad: float32 [768, 3, 768], P('dp', None, 'tensor')
- w_out_grad: float32 [768, 768], P('tensor', 'dp')
- w_fc_grad: float32 [768, 3072], P('dp', 'tensor')
- w_proj_grad: float32 [3072, 768], P('tensor', 'dp')
- ln1_gain_grad: float32 [768], P('dp')
- ln1_bias_grad: float32 [768], P('dp')
- ln2_gain_grad: float32 [768], P('dp')
- ln2_bias_grad: float32 [768], P('dp')
Inputs may be any that keep to these rules, and one draw needn't show every extreme that they name: `lengths`: row g lists the token counts of group g's 8 continuations in order after its 512-token prompt; each row sums to 2048 and its largest entry is exactly 512.
All inputs are finite; a program needn't handle non-finite values.
Results may differ from a plain program's by a relative error of at most 0.019.
The roundings to bfloat16 on the way count: a program that leaves them out, or rounds other values in their place, can miss the bound.
Values may be sent and summed in bfloat16 or wider, within the bound.
A program may use at most 192 MiB of HBM per device.

v0:
```python
import jax
import jax.numpy as jnp
from jax import lax
from jax.sharding import PartitionSpec as P

HEAD = 64
PROMPT = 512


def normalize(values):
    mean = jnp.mean(values, axis=-1, keepdims=True)
    centred = values - mean
    spread = jnp.mean(centred * centred, axis=-1, keepdims=True)
    factor = lax.rsqrt(spread + 1e-05)
    return (centred * factor, factor)


def norm_back(grad_out, normed, factor, gain):
    scaled = grad_out * gain
    first = jnp.mean(scaled, axis=-1, keepdims=True)
    second = jnp.mean(scaled * normed, axis=-1, keepdims=True)
    return factor * (scaled - first - normed * second)


def gelu_tanh(values):
    return jax.nn.gelu(values, approximate=True)


def inner_rows(left, right):
    return lax.dot_general(
        left, right, (((0,), (0,)), ((), ())), preferred_element_type=jnp.float32
    )


def times_trans(left, right):
    return lax.dot_general(
        left, right, (((1,), (1,)), ((), ())), preferred_element_type=jnp.float32
    )


def segment_ids(lengths, total):
    ends = PROMPT + jnp.cumsum(lengths[0])
    places = jnp.arange(total, dtype=jnp.int32)
    passed = jnp.sum((places[:, None] >= ends[None, :]).astype(jnp.int32), axis=1)
    return (places, jnp.where(places < PROMPT, -1, passed))


def visible(query_pos, query_seg, key_pos, key_seg):
    causal = key_pos[None, :] <= query_pos[:, None]
    shared = (key_seg[None, :] < 0) | (key_seg[None, :] == query_seg[:, None])
    return (causal & shared)[None]


def attend(queries, keys, values, places, segs, block, scale):
    count = queries.shape[0] // block

    def one(index):
        start = index * block
        query = lax.dynamic_slice_in_dim(queries, start, block, 0)
        mask = visible(
            lax.dynamic_slice_in_dim(places, start, block, 0),
            lax.dynamic_slice_in_dim(segs, start, block, 0),
            places,
            segs,
        )
        raw = jnp.einsum("qhd,khd->hqk", query, keys, preferred_element_type=jnp.float32) * scale
        magnitude = jnp.where(mask, jnp.abs(raw), -1e30)
        top = jnp.max(magnitude, axis=-1, keepdims=True)
        expo = jnp.where(mask, jnp.exp(magnitude - top), 0.0)
        total = jnp.sum(expo, axis=-1, keepdims=True)
        weights = (jnp.sign(raw) * (expo / total)).astype(jnp.bfloat16)
        mixed = jnp.einsum("hqk,khd->qhd", weights, values, preferred_element_type=jnp.float32)
        return (mixed.astype(jnp.bfloat16), (top + jnp.log(total))[..., 0])

    mixed, sums = lax.map(one, jnp.arange(count, dtype=jnp.int32))
    return (mixed.reshape(queries.shape[0], -1), sums)


def attend_back(queries, keys, values, grad_mixed, sums, places, segs, block, scale):
    count = queries.shape[0] // block

    def step(carry, inputs):
        key_grad, value_grad = carry
        index, lse_block = inputs
        start = index * block
        query = lax.dynamic_slice_in_dim(queries, start, block, 0)
        grad_block = lax.dynamic_slice_in_dim(grad_mixed, start, block, 0)
        mask = visible(
            lax.dynamic_slice_in_dim(places, start, block, 0),
            lax.dynamic_slice_in_dim(segs, start, block, 0),
            places,
            segs,
        )
        raw = jnp.einsum("qhd,khd->hqk", query, keys, preferred_element_type=jnp.float32) * scale
        prob = jnp.where(mask, jnp.exp(jnp.abs(raw) - lse_block[..., None]), 0.0)
        signed = jnp.sign(raw) * prob
        rounded = signed.astype(jnp.bfloat16)
        value_grad = value_grad + jnp.einsum(
            "hqk,qhd->khd", rounded, grad_block, preferred_element_type=jnp.float32
        )
        weight_grad = jnp.einsum(
            "qhd,khd->hqk", grad_block, values, preferred_element_type=jnp.float32
        )
        inner = jnp.sum(signed * weight_grad, axis=-1, keepdims=True)
        score_grad = (prob * weight_grad - signed * inner).astype(jnp.bfloat16)
        query_grad = (
            jnp.einsum("hqk,khd->qhd", score_grad, keys, preferred_element_type=jnp.float32) * scale
        )
        key_grad = (
            key_grad
            + jnp.einsum("hqk,qhd->khd", score_grad, query, preferred_element_type=jnp.float32)
            * scale
        )
        return ((key_grad, value_grad), query_grad)

    zeros = jnp.zeros(keys.shape, jnp.float32)
    (key_grad, value_grad), query_grad = lax.scan(
        step, (zeros, zeros), (jnp.arange(count, dtype=jnp.int32), sums)
    )
    return (query_grad.reshape(keys.shape), key_grad, value_grad)


def on_device(
    tokens, cotangent, lengths, w_qkv, w_out, w_fc, w_proj, ln1_gain, ln1_bias, ln2_gain, ln2_bias
):
    rows = tokens.shape[0]
    group = rows * lax.axis_size("tensor")
    block = group // max(1, group // 512)
    scale = HEAD ** (-0.5)
    pieces = (w_qkv, w_out, w_fc, w_proj, ln1_gain, ln1_bias, ln2_gain, ln2_bias)
    qkv_full, out_full, fc_full, proj_full, gain1, bias1, gain2, bias2 = (
        lax.all_gather(pieces[0], "dp", axis=0, tiled=True),
        lax.all_gather(pieces[1], "dp", axis=1, tiled=True),
        lax.all_gather(pieces[2], "dp", axis=0, tiled=True),
        lax.all_gather(pieces[3], "dp", axis=1, tiled=True),
        lax.all_gather(pieces[4], "dp", axis=0, tiled=True),
        lax.all_gather(pieces[5], "dp", axis=0, tiled=True),
        lax.all_gather(pieces[6], "dp", axis=0, tiled=True),
        lax.all_gather(pieces[7], "dp", axis=0, tiled=True),
    )
    gain1 = gain1.astype(jnp.float32)
    bias1 = bias1.astype(jnp.float32)
    gain2 = gain2.astype(jnp.float32)
    bias2 = bias2.astype(jnp.float32)
    width = qkv_full.shape[0]
    local = qkv_full.shape[2]
    heads = local // HEAD
    qkv_mat = qkv_full.reshape(width, 3 * local)
    places, segs = segment_ids(lengths, group)
    inputs = tokens.astype(jnp.float32)
    normed1, factor1 = normalize(inputs)
    lowered1 = (normed1 * gain1 + bias1).astype(jnp.bfloat16)
    all_norm1 = lax.all_gather(lowered1, "tensor", axis=0, tiled=True)
    projected = jnp.dot(all_norm1, qkv_mat, preferred_element_type=jnp.float32).astype(jnp.bfloat16)
    projected = projected.reshape(group, 3, heads, HEAD)
    queries = projected[:, 0]
    keys = projected[:, 1]
    values = projected[:, 2]
    mixed, sums = attend(queries, keys, values, places, segs, block, scale)
    part = mixed
    resid = inputs + lax.psum_scatter(
        jnp.dot(part, out_full, preferred_element_type=jnp.float32).astype(jnp.bfloat16),
        "tensor",
        scatter_dimension=0,
        tiled=True,
    ).astype(jnp.float32)
    normed2, factor2 = normalize(resid)
    lowered2 = (normed2 * gain2 + bias2).astype(jnp.bfloat16)
    all_norm2 = lax.all_gather(lowered2, "tensor", axis=0, tiled=True)
    hidden_pre = jnp.dot(all_norm2, fc_full, preferred_element_type=jnp.float32)
    hidden, gelu_pull = jax.vjp(gelu_tanh, hidden_pre)
    hidden_low = hidden.astype(jnp.bfloat16)
    part = hidden_low
    mlp_rows = lax.psum_scatter(
        jnp.dot(part, proj_full, preferred_element_type=jnp.float32).astype(jnp.bfloat16),
        "tensor",
        scatter_dimension=0,
        tiled=True,
    ).astype(jnp.float32)
    block_out = (resid + mlp_rows).astype(jnp.bfloat16)
    grad_all = lax.all_gather(cotangent, "tensor", axis=0, tiled=True)
    hidden_grad = times_trans(grad_all, proj_full)
    proj_grad = inner_rows(hidden_low, grad_all)
    pre_low = gelu_pull(hidden_grad)[0].astype(jnp.bfloat16)
    fc_grad = inner_rows(all_norm2, pre_low)
    part = pre_low
    norm2_grad = lax.psum_scatter(
        times_trans(part, fc_full).astype(jnp.bfloat16), "tensor", scatter_dimension=0, tiled=True
    ).astype(jnp.float32)
    gain2_part = jnp.sum(norm2_grad * normed2, axis=0)
    bias2_part = jnp.sum(norm2_grad, axis=0)
    resid_grad = cotangent.astype(jnp.float32) + norm_back(norm2_grad, normed2, factor2, gain2)
    resid_low = resid_grad.astype(jnp.bfloat16)
    resid_all = lax.all_gather(resid_low, "tensor", axis=0, tiled=True)
    out_grad = inner_rows(mixed, resid_all)
    mixed_grad = times_trans(resid_all, out_full).astype(jnp.bfloat16).reshape(group, heads, HEAD)
    query_grad, key_grad, value_grad = attend_back(
        queries, keys, values, mixed_grad, sums, places, segs, block, scale
    )
    qkv_grad_low = (
        jnp.stack([query_grad, key_grad, value_grad], axis=1)
        .astype(jnp.bfloat16)
        .reshape(group, 3 * local)
    )
    qkv_grad = inner_rows(all_norm1, qkv_grad_low).reshape(width, 3, local)
    part = qkv_grad_low
    norm1_grad = lax.psum_scatter(
        times_trans(part, qkv_mat).astype(jnp.bfloat16), "tensor", scatter_dimension=0, tiled=True
    ).astype(jnp.float32)
    gain1_part = jnp.sum(norm1_grad * normed1, axis=0)
    bias1_part = jnp.sum(norm1_grad, axis=0)
    input_grad = (resid_grad + norm_back(norm1_grad, normed1, factor1, gain1)).astype(jnp.bfloat16)
    qkv_sum, out_sum, fc_sum, proj_sum, gain1_share, bias1_share, gain2_share, bias2_share = (
        lax.psum_scatter(qkv_grad, "dp", scatter_dimension=0, tiled=True),
        lax.psum_scatter(out_grad, "dp", scatter_dimension=1, tiled=True),
        lax.psum_scatter(fc_grad, "dp", scatter_dimension=0, tiled=True),
        lax.psum_scatter(proj_grad, "dp", scatter_dimension=1, tiled=True),
        lax.psum_scatter(gain1_part, "dp", scatter_dimension=0, tiled=True),
        lax.psum_scatter(bias1_part, "dp", scatter_dimension=0, tiled=True),
        lax.psum_scatter(gain2_part, "dp", scatter_dimension=0, tiled=True),
        lax.psum_scatter(bias2_part, "dp", scatter_dimension=0, tiled=True),
    )
    gain1_sum, bias1_sum, gain2_sum, bias2_sum = lax.psum(
        (gain1_share, bias1_share, gain2_share, bias2_share), "tensor"
    )
    return (
        block_out,
        input_grad,
        qkv_sum,
        out_sum,
        fc_sum,
        proj_sum,
        gain1_sum,
        bias1_sum,
        gain2_sum,
        bias2_sum,
    )


def solution(mesh):
    placed = (
        P(("dp", "tensor"), None),
        P(("dp", "tensor"), None),
        P("dp", None),
        P("dp", None, "tensor"),
        P("tensor", "dp"),
        P("dp", "tensor"),
        P("tensor", "dp"),
        P("dp"),
        P("dp"),
        P("dp"),
        P("dp"),
    )
    return jax.shard_map(
        on_device,
        mesh=mesh,
        in_specs=placed,
        out_specs=(
            P(("dp", "tensor"), None),
            P(("dp", "tensor"), None),
            P("dp", None, "tensor"),
            P("tensor", "dp"),
            P("dp", "tensor"),
            P("tensor", "dp"),
            P("dp"),
            P("dp"),
            P("dp"),
            P("dp"),
        ),
        check_vma=False,
    )
```

profile of v0, /device:TPU:0, one launch (start us, length us, event | category | flops | bytes accessed | tf_op | source)
XLA Modules:
  0.0 1164.4 jit_solution(4583404668944278764)
XLA Ops:
  13.4 23.9 %all-reduce.10 = (bf16[768]{0:T(1024)(128)(2,1)}, bf16[768]{0:T(1024)(128)(2,1)}, bf16[768]{0:T(1024)(128)(2,1)S(1)}, bf16[768]{0:T(1024)(128)(2,1)S(1)}) all-reduce(bf16[768]{0:T(1024)(128)(2,1)S(1)} %dynamic-update-slice.3, bf16[768]{0:T(1024)(128)(2,1)S(1)} %dynamic-update-slice.2, ...), channel_id=1, replica_groups=mesh['dp'=8,'tensor'=4] {'dp'}, use_global_device_ids=true, to_apply=%add.3 | all-reduce | flops 3072 | bytes 12288
  43.6 35.5 %all_gather.39 = bf16[768,3,192]{2,1,0:T(4,128)(2,1)S(1)} all-gather(bf16[96,3,192]{2,1,0:T(4,128)(2,1)S(1)} %copy.32), channel_id=1, replica_groups=mesh['dp'=8,'tensor'=4] {'dp'}, dimensions={0}, use_global_device_ids=true | all-gather | bytes 995328 | tf_op jit(solution)/shard_map/all_gather | solution.py:132
  80.1 33.6 %all_gather.40 = bf16[192,768]{0,1:T(8,128)(2,1)} all-gather(bf16[192,96]{0,1:T(8,128)(2,1)S(1)} %copy.35), channel_id=1, replica_groups=mesh['dp'=8,'tensor'=4] {'dp'}, dimensions={1}, use_global_device_ids=true | all-gather | bytes 331776 | tf_op jit(solution)/shard_map/all_gather | solution.py:133
  119.7 122.1 %while.29 = (s32[]{:T(128)}, bf16[5,512,3,64]{1,3,2,0:T(8,128)(2,1)S(1)}, f32[5,3,512]{2,1,0:T(4,128)S(1)}, s32[5]{0:T(128)S(1)}, bf16[2560,3,64]{0,2,1:T(8,128)...) while((s32[]{:T(128)}, ...), condition=%wide.region_7.8_spmd.clone, body=%wide.region_4.7_spmd.clone.sunk | while | flops 1086686208 | bytes 54895824 | solution.py:75
  133.5 10.6 fusion.127
  248.8 40.7 %reduce-scatter.11.cloned.1.call-done = bf16[640,768]{1,0:T(8,128)(2,1)} async-done(((bf16[2560,768]{1,0:T(8,128)(2,1)}), bf16[640,768]{1,0:T(8,128)(2,1)}) %reduce-scatter.11.cloned.1.call-update) | async-done | bytes 983056 | tf_op jit(solution)/shard_map/reduce_scatter | solution.py:161
  294.4 28.8 %all-gather.15.cloned.1.call-done = bf16[2560,768]{1,0:T(8,128)(2,1)} async-done(((bf16[640,768]{1,0:T(8,128)(2,1)}), bf16[2560,768]{1,0:T(8,128)(2,1)}) %all-gather.15.cloned.1.call-update) | async-done | bytes 3932176 | tf_op jit(solution)/shard_map/all_gather | solution.py:181
  332.1 34.7 %all-gather.11.cloned.1.call-done = bf16[768,768]{1,0:T(8,128)(2,1)} async-done(((bf16[96,768]{1,0:T(8,128)(2,1)}), bf16[768,768]{1,0:T(8,128)(2,1)}) %all-gather.11.cloned.1.call-update) | async-done | bytes 1179664 | tf_op jit(solution)/shard_map/all_gather | solution.py:134
  366.7 33.4 %all-gather.9.cloned.1.call-done = bf16[2560,768]{1,0:T(8,128)(2,1)} async-done(((bf16[640,768]{1,0:T(8,128)(2,1)}), bf16[2560,768]{1,0:T(8,128)(2,1)}) %all-gather.9.cloned.1.call-update) | async-done | bytes 3932176 | tf_op jit(solution)/shard_map/all_gather | solution.py:169
  400.1 13.6 %fusion.43 = (bf16[2560,768]{1,0:T(8,128)(2,1)S(1)}, f32[2560,768]{1,0:T(8,128)}) fusion(f32[2560,768]{1,0:T(8,128)} %fusion.75, bf16[2560,768]{1,0:T(8,128)(2,1)} %all-gather.9.cloned.1.call-done, bf16[768,768]{1,0:T(8,128)(2,1)} %all-gather.11.cloned.1.call-done), kind=kOutput, calls=%fused_computation.55 | convolution fusion | flops 3059220480 | bytes 24772608 | tf_op jit(solution)/shard_map/dot_general | solution.py:170
  421.0 42.6 %reduce-scatter.15.cloned.1.call-done = bf16[640,768]{1,0:T(8,128)(2,1)} async-done(((bf16[2560,768]{1,0:T(8,128)(2,1)}), bf16[640,768]{1,0:T(8,128)(2,1)}) %reduce-scatter.15.cloned.1.call-update) | async-done | bytes 983056 | tf_op jit(solution)/shard_map/reduce_scatter | solution.py:187
  470.5 32.9 %all-gather.17.cloned.1.call-done = bf16[2560,768]{1,0:T(8,128)(2,1)} async-done(((bf16[640,768]{1,0:T(8,128)(2,1)}), bf16[2560,768]{1,0:T(8,128)(2,1)}) %all-gather.17.cloned.1.call-update) | async-done | bytes 3932176 | tf_op jit(solution)/shard_map/all_gather | solution.py:194
  512.9 323.7 %while.30 = (s32[]{:T(128)}, f32[2560,3,64]{0,2,1:T(8,128)}, f32[2560,3,64]{0,2,1:T(8,128)}, bf16[5,512,3,64]{1,0,3,2:T(8,128)(2,1)}, s32[5]{0:T(128)S(1)}, /*in...) while((s32[]{:T(128)}, f32[2560,3,64]{0,2,1:T(8,128)}, ...), condition=%wide.region_17.18_spmd.clone.clone, body=%wide.region_15.17_spmd.clone.clone.sunk | while | flops 2622784512 | bytes 218457456 | solution.py:117
  519.5 12.2 %fusion.139 = f32[2560,3,64]{0,2,1:T(8,128)} fusion(f32[3,512,2560]{2,1,0:T(8,128)S(1)} %fusion.137, f32[3,512]{1,0:T(4,128)S(1)} %dynamic-slice_bitcast_fusion.2, pred[512,2560]{1,0:T(8,128)(4,1)S(1)} %or_and_fusion.5, f32[2560,3,64]{0,2,1:T(8,128)} %get-tuple-element.492, pred[]{:T(512)S(6)} %compare.3, ...), kind=kOutput, calls=%fused_computation.30.clone.1 | convolution fusion | flops 531824640 | bytes 21174276 | tf_op jit(solution)/shard_map/while/body/eval_jaxpr/hqk,qhd->khd/dot_general | solution.py:98
  531.7 15.0 %multiply_reduce_fusion.3 = (f32[3,512]{1,0:T(4,128)S(1)}, f32[3,512,2560]{2,1,0:T(8,128)}) fusion(f32[3,512,2560]{2,1,0:T(8,128)S(1)} %fusion.137, f32[3,512]{1,0:T(4,128)S(1)} %dynamic-slice_bitcast_fusion.2, pred[512,2560]{1,0:T(8,128)(4,1)S(1)} %or_and_fusion.5, bf16[2560,3,64]{0,2,1:T(8,128)(2,1)S(1)} %copy-done.12, ...), kind=kOutput, calls=%fused_computation.19.clone.1 | convolution fusion | flops 534772224 | bytes 33959940 | tf_op jit(solution)/shard_map/while/body/eval_jaxpr/qhd,khd->hqk/dot_general | solution.py:101
  546.7 15.2 %subtract_convert_fusion.2 = bf16[3,512,2560]{2,1,0:T(8,128)(2,1)S(1)} fusion(f32[3,512,2560]{2,1,0:T(8,128)} %get-tuple-element.433, f32[3,512,2560]{2,1,0:T(8,128)} %copy-done, f32[3,512]{1,0:T(4,128)S(1)} %get-tuple-element.434, f32[3,512]{1,0:T(4,128)S(1)} %dynamic-slice_bitcast_fusion.2, pred[512,2560]{1,0:T(8,128)(4,1)S(1)} %or_and_fusion.5), kind=kLoop, calls=%fused_computation.18.clone.1 | loop fusion | flops 39321600 | bytes 40644608 | tf_op jit(solution)/shard_map/while/body/eval_jaxpr/convert_element_type | solution.py:105
  582.4 14.4 %fusion.139 = f32[2560,3,64]{0,2,1:T(8,128)} fusion(f32[3,512,2560]{2,1,0:T(8,128)S(1)} %fusion.137, f32[3,512]{1,0:T(4,128)S(1)} %dynamic-slice_bitcast_fusion.2, pred[512,2560]{1,0:T(8,128)(4,1)S(1)} %or_and_fusion.5, f32[2560,3,64]{0,2,1:T(8,128)} %get-tuple-element.492, pred[]{:T(512)S(6)} %compare.3, ...), kind=kOutput, calls=%fused_computation.30.clone.1 | convolution fusion | flops 531824640 | bytes 21174276 | tf_op jit(solution)/shard_map/while/body/eval_jaxpr/hqk,qhd->khd/dot_general | solution.py:98
  596.8 15.0 %multiply_reduce_fusion.3 = (f32[3,512]{1,0:T(4,128)S(1)}, f32[3,512,2560]{2,1,0:T(8,128)}) fusion(f32[3,512,2560]{2,1,0:T(8,128)S(1)} %fusion.137, f32[3,512]{1,0:T(4,128)S(1)} %dynamic-slice_bitcast_fusion.2, pred[512,2560]{1,0:T(8,128)(4,1)S(1)} %or_and_fusion.5, bf16[2560,3,64]{0,2,1:T(8,128)(2,1)S(1)} %copy-done.12, ...), kind=kOutput, calls=%fused_computation.19.clone.1 | convolution fusion | flops 534772224 | bytes 33959940 | tf_op jit(solution)/shard_map/while/body/eval_jaxpr/qhd,khd->hqk/dot_general | solution.py:101
  611.8 15.2 %subtract_convert_fusion.2 = bf16[3,512,2560]{2,1,0:T(8,128)(2,1)S(1)} fusion(f32[3,512,2560]{2,1,0:T(8,128)} %get-tuple-element.433, f32[3,512,2560]{2,1,0:T(8,128)} %copy-done, f32[3,512]{1,0:T(4,128)S(1)} %get-tuple-element.434, f32[3,512]{1,0:T(4,128)S(1)} %dynamic-slice_bitcast_fusion.2, pred[512,2560]{1,0:T(8,128)(4,1)S(1)} %or_and_fusion.5), kind=kLoop, calls=%fused_computation.18.clone.1 | loop fusion | flops 39321600 | bytes 40644608 | tf_op jit(solution)/shard_map/while/body/eval_jaxpr/convert_element_type | solution.py:105
  647.4 14.4 %fusion.139 = f32[2560,3,64]{0,2,1:T(8,128)} fusion(f32[3,512,2560]{2,1,0:T(8,128)S(1)} %fusion.137, f32[3,512]{1,0:T(4,128)S(1)} %dynamic-slice_bitcast_fusion.2, pred[512,2560]{1,0:T(8,128)(4,1)S(1)} %or_and_fusion.5, f32[2560,3,64]{0,2,1:T(8,128)} %get-tuple-element.492, pred[]{:T(512)S(6)} %compare.3, ...), kind=kOutput, calls=%fused_computation.30.clone.1 | convolution fusion | flops 531824640 | bytes 21174276 | tf_op jit(solution)/shard_map/while/body/eval_jaxpr/hqk,qhd->khd/dot_general | solution.py:98
  661.8 15.0 %multiply_reduce_fusion.3 = (f32[3,512]{1,0:T(4,128)S(1)}, f32[3,512,2560]{2,1,0:T(8,128)}) fusion(f32[3,512,2560]{2,1,0:T(8,128)S(1)} %fusion.137, f32[3,512]{1,0:T(4,128)S(1)} %dynamic-slice_bitcast_fusion.2, pred[512,2560]{1,0:T(8,128)(4,1)S(1)} %or_and_fusion.5, bf16[2560,3,64]{0,2,1:T(8,128)(2,1)S(1)} %copy-done.12, ...), kind=kOutput, calls=%fused_computation.19.clone.1 | convolution fusion | flops 534772224 | bytes 33959940 | tf_op jit(solution)/shard_map/while/body/eval_jaxpr/qhd,khd->hqk/dot_general | solution.py:101
  676.8 15.2 %subtract_convert_fusion.2 = bf16[3,512,2560]{2,1,0:T(8,128)(2,1)S(1)} fusion(f32[3,512,2560]{2,1,0:T(8,128)} %get-tuple-element.433, f32[3,512,2560]{2,1,0:T(8,128)} %copy-done, f32[3,512]{1,0:T(4,128)S(1)} %get-tuple-element.434, f32[3,512]{1,0:T(4,128)S(1)} %dynamic-slice_bitcast_fusion.2, pred[512,2560]{1,0:T(8,128)(4,1)S(1)} %or_and_fusion.5), kind=kLoop, calls=%fused_computation.18.clone.1 | loop fusion | flops 39321600 | bytes 40644608 | tf_op jit(solution)/shard_map/while/body/eval_jaxpr/convert_element_type | solution.py:105
  712.5 14.4 %fusion.139 = f32[2560,3,64]{0,2,1:T(8,128)} fusion(f32[3,512,2560]{2,1,0:T(8,128)S(1)} %fusion.137, f32[3,512]{1,0:T(4,128)S(1)} %dynamic-slice_bitcast_fusion.2, pred[512,2560]{1,0:T(8,128)(4,1)S(1)} %or_and_fusion.5, f32[2560,3,64]{0,2,1:T(8,128)} %get-tuple-element.492, pred[]{:T(512)S(6)} %compare.3, ...), kind=kOutput, calls=%fused_computation.30.clone.1 | convolution fusion | flops 531824640 | bytes 21174276 | tf_op jit(solution)/shard_map/while/body/eval_jaxpr/hqk,qhd->khd/dot_general | solution.py:98
  726.9 15.0 %multiply_reduce_fusion.3 = (f32[3,512]{1,0:T(4,128)S(1)}, f32[3,512,2560]{2,1,0:T(8,128)}) fusion(f32[3,512,2560]{2,1,0:T(8,128)S(1)} %fusion.137, f32[3,512]{1,0:T(4,128)S(1)} %dynamic-slice_bitcast_fusion.2, pred[512,2560]{1,0:T(8,128)(4,1)S(1)} %or_and_fusion.5, bf16[2560,3,64]{0,2,1:T(8,128)(2,1)S(1)} %copy-done.12, ...), kind=kOutput, calls=%fused_computation.19.clone.1 | convolution fusion | flops 534772224 | bytes 33959940 | tf_op jit(solution)/shard_map/while/body/eval_jaxpr/qhd,khd->hqk/dot_general | solution.py:101
  741.9 15.2 %subtract_convert_fusion.2 = bf16[3,512,2560]{2,1,0:T(8,128)(2,1)S(1)} fusion(f32[3,512,2560]{2,1,0:T(8,128)} %get-tuple-element.433, f32[3,512,2560]{2,1,0:T(8,128)} %copy-done, f32[3,512]{1,0:T(4,128)S(1)} %get-tuple-element.434, f32[3,512]{1,0:T(4,128)S(1)} %dynamic-slice_bitcast_fusion.2, pred[512,2560]{1,0:T(8,128)(4,1)S(1)} %or_and_fusion.5), kind=kLoop, calls=%fused_computation.18.clone.1 | loop fusion | flops 39321600 | bytes 40644608 | tf_op jit(solution)/shard_map/while/body/eval_jaxpr/convert_element_type | solution.py:105
  777.6 14.4 %fusion.139 = f32[2560,3,64]{0,2,1:T(8,128)} fusion(f32[3,512,2560]{2,1,0:T(8,128)S(1)} %fusion.137, f32[3,512]{1,0:T(4,128)S(1)} %dynamic-slice_bitcast_fusion.2, pred[512,2560]{1,0:T(8,128)(4,1)S(1)} %or_and_fusion.5, f32[2560,3,64]{0,2,1:T(8,128)} %get-tuple-element.492, pred[]{:T(512)S(6)} %compare.3, ...), kind=kOutput, calls=%fused_computation.30.clone.1 | convolution fusion | flops 531824640 | bytes 21174276 | tf_op jit(solution)/shard_map/while/body/eval_jaxpr/hqk,qhd->khd/dot_general | solution.py:98
  792.0 15.0 %multiply_reduce_fusion.3 = (f32[3,512]{1,0:T(4,128)S(1)}, f32[3,512,2560]{2,1,0:T(8,128)}) fusion(f32[3,512,2560]{2,1,0:T(8,128)S(1)} %fusion.137, f32[3,512]{1,0:T(4,128)S(1)} %dynamic-slice_bitcast_fusion.2, pred[512,2560]{1,0:T(8,128)(4,1)S(1)} %or_and_fusion.5, bf16[2560,3,64]{0,2,1:T(8,128)(2,1)S(1)} %copy-done.12, ...), kind=kOutput, calls=%fused_computation.19.clone.1 | convolution fusion | flops 534772224 | bytes 33959940 | tf_op jit(solution)/shard_map/while/body/eval_jaxpr/qhd,khd->hqk/dot_general | solution.py:101
  807.0 15.2 %subtract_convert_fusion.2 = bf16[3,512,2560]{2,1,0:T(8,128)(2,1)S(1)} fusion(f32[3,512,2560]{2,1,0:T(8,128)} %get-tuple-element.433, f32[3,512,2560]{2,1,0:T(8,128)} %copy-done, f32[3,512]{1,0:T(4,128)S(1)} %get-tuple-element.434, f32[3,512]{1,0:T(4,128)S(1)} %dynamic-slice_bitcast_fusion.2, pred[512,2560]{1,0:T(8,128)(4,1)S(1)} %or_and_fusion.5), kind=kLoop, calls=%fused_computation.18.clone.1 | loop fusion | flops 39321600 | bytes 40644608 | tf_op jit(solution)/shard_map/while/body/eval_jaxpr/convert_element_type | solution.py:105
  893.8 37.1 %all-reduce.8 = (f32[768]{0:T(1024)S(1)}, f32[768]{0:T(1024)S(1)}, f32[768]{0:T(1024)S(1)}, f32[768]{0:T(1024)S(1)}) all-reduce(f32[768]{0:T(1024)S(1)} %get-tuple-element.224, f32[768]{0:T(1024)S(1)} %get-tuple-element.229, f32[768]{0:T(1024)S(1)} %copy-done.34, ...), channel_id=10, replica_groups=mesh['dp'=8,'tensor'=4] {'dp'}, use_global_device_ids=true, to_apply=%region_26.27.clone | all-reduce | flops 3072 | bytes 24576
  941.8 68.8 %reduce-scatter.21.cloned.1.call-done = f32[96,768]{1,0:T(8,128)} async-done(((f32[768,768]{1,0:T(8,128)}), f32[96,768]{1,0:T(8,128)}) %reduce-scatter.21.cloned.1.call-update) | async-done | bytes 294928 | tf_op jit(solution)/shard_map/reduce_scatter | solution.py:216
  1010.6 73.1 %reduce-scatter.23.cloned.1.call-done = f32[768,96]{0,1:T(8,128)} async-done(((f32[768,768]{0,1:T(8,128)}), f32[768,96]{0,1:T(8,128)}) %reduce-scatter.23.cloned.1.call-update) | async-done | bytes 294928 | tf_op jit(solution)/shard_map/reduce_scatter | solution.py:217
  1083.8 73.1 %reduce-scatter.19.cloned.1.call-done = f32[96,3,192]{2,0,1:T(8,128)} async-done(((f32[768,3,192]{2,0,1:T(8,128)}), f32[96,3,192]{2,0,1:T(8,128)}) %reduce-scatter.19.cloned.1.call-update) | async-done | bytes 221200 | tf_op jit(solution)/shard_map/reduce_scatter | solution.py:214
  (316 shorter events, 335.3 us)
Async XLA Ops:
  8.0 35.1 %copy-start.40 = (s32[1,8]{1,0:T(1,128)S(1)}, s32[1,8]{1,0:T(1,128)}, u32[]{:S(2)}) copy-start(s32[1,8]{1,0:T(1,128)} %param.17) | copy-start | bytes 100
  8.0 35.3 %copy-start.29 = (bf16[192,96]{1,0:T(8,128)(2,1)S(1)}, bf16[192,96]{1,0:T(8,128)(2,1)}, u32[]{:S(2)}) copy-start(bf16[192,96]{1,0:T(8,128)(2,1)} %param.19) | copy-start | bytes 110596
  8.0 35.4 %copy-start.16 = (bf16[96,3,192]{2,0,1:T(8,128)(2,1)S(1)}, bf16[96,3,192]{2,0,1:T(8,128)(2,1)}, u32[]{:S(2)}) copy-start(bf16[96,3,192]{2,0,1:T(8,128)(2,1)} %param.18) | copy-start | bytes 331780
  8.0 105.7 %all-gather.7.cloned.1.call-start = ((), (), s32[]{:S(2)}) async-start(), calls=%async_computation.8 | async-start | bytes 4915200 | tf_op jit(solution)/shard_map/all_gather | solution.py:153
  43.0 246.5 %reduce-scatter.11.cloned.1.call-start = ((), (), s32[]{:S(2)}) async-start(), calls=%async_computation.9 | async-start | bytes 4915200 | tf_op jit(solution)/shard_map/reduce_scatter | solution.py:161
  80.0 38.3 %copy-start.14 = (bf16[768,3,192]{0,2,1:T(8,128)(2,1)}, bf16[768,3,192]{0,2,1:T(8,128)(2,1)S(1)}, u32[]{:S(2)}) copy-start(bf16[768,3,192]{0,2,1:T(8,128)(2,1)S(1)} %copy.33) | copy-start | bytes 2654212
  246.9 42.6 %copy-start.1 = (bf16[640,768]{1,0:T(8,128)(2,1)S(1)}, bf16[640,768]{1,0:T(8,128)(2,1)}, u32[]{:S(2)}) copy-start(bf16[640,768]{1,0:T(8,128)(2,1)} %param.15) | copy-start | bytes 2949124
  247.0 47.5 %all-gather.13.cloned.1.call-start = ((), (), s32[]{:S(2)}) async-start(), calls=%async_computation.12 | async-start | bytes 1327104 | tf_op jit(solution)/shard_map/all_gather | solution.py:135
  247.5 75.7 %all-gather.15.cloned.1.call-start = ((), (), s32[]{:S(2)}) async-start(), calls=%async_computation.14 | async-start | bytes 4915200 | tf_op jit(solution)/shard_map/all_gather | solution.py:181
  248.1 118.6 %all-gather.11.cloned.1.call-start = ((), (), s32[]{:S(2)}) async-start(), calls=%async_computation.11 | async-start | bytes 1327104 | tf_op jit(solution)/shard_map/all_gather | solution.py:134
  248.7 151.4 %all-gather.9.cloned.1.call-start = ((), (), s32[]{:S(2)}) async-start(), calls=%async_computation.10 | async-start | bytes 4915200 | tf_op jit(solution)/shard_map/all_gather | solution.py:169
  248.8 217.6 %copy-start.21 = (f32[768]{0:T(1024)}, f32[768]{0:T(1024)S(1)}, u32[]{:S(2)}) copy-start(f32[768]{0:T(1024)S(1)} %convert_element_type.109) | copy-start | bytes 9220
  291.2 175.2 %copy-start.17 = (f32[640]{0:T(1024)}, f32[640]{0:T(1024)S(1)}, u32[]{:S(2)}) copy-start(f32[640]{0:T(1024)S(1)} %broadcast_multiply_fusion.4) | copy-start | bytes 7684
  292.9 173.5 %copy-start.23 = (f32[640]{0:T(1024)}, f32[640]{0:T(1024)S(1)}, u32[]{:S(2)}) copy-start(f32[640]{0:T(1024)S(1)} %add_rsqrt_fusion) | copy-start | bytes 7684
  294.4 169.2 %reduce-scatter.15.cloned.1.call-start = ((), (), s32[]{:S(2)}) async-start(), calls=%async_computation.15 | async-start | bytes 4915200 | tf_op jit(solution)/shard_map/reduce_scatter | solution.py:187
  400.1 15.6 %copy-start.39 = (bf16[768,768]{1,0:T(8,128)(2,1)S(1)}, bf16[768,768]{1,0:T(8,128)(2,1)}, u32[]{:S(2)}) copy-start(bf16[768,768]{1,0:T(8,128)(2,1)} %all-gather.11.cloned.1.call-done) | copy-start | bytes 3538948
  420.5 82.9 %all-gather.17.cloned.1.call-start = ((), (), s32[]{:S(2)}) async-start(), calls=%async_computation.16 | async-start | bytes 4915200 | tf_op jit(solution)/shard_map/all_gather | solution.py:194
  470.4 416.2 %reduce-scatter.25.cloned.1.call-start = ((), (), s32[]{:S(2)}) async-start(), calls=%async_computation.21 | async-start | bytes 884736
  508.3 383.3 %reduce-scatter.17.cloned.1.call-start = ((), (), s32[]{:S(2)}) async-start(), calls=%async_computation.17 | async-start | bytes 4915200 | tf_op jit(solution)/shard_map/reduce_scatter | solution.py:207
  582.4 14.4 %copy-start = (f32[3,512,2560]{2,1,0:T(8,128)}, f32[3,512,2560]{2,1,0:T(8,128)S(1)}, u32[]{:S(2)}) copy-start(f32[3,512,2560]{2,1,0:T(8,128)S(1)} %fusion.137) | copy-start | bytes 47185924 | tf_op jit(solution)/shard_map/while
  647.4 14.4 %copy-start = (f32[3,512,2560]{2,1,0:T(8,128)}, f32[3,512,2560]{2,1,0:T(8,128)S(1)}, u32[]{:S(2)}) copy-start(f32[3,512,2560]{2,1,0:T(8,128)S(1)} %fusion.137) | copy-start | bytes 47185924 | tf_op jit(solution)/shard_map/while
  848.7 88.9 %reduce-scatter.13.cloned.1.call-start = ((), (), s32[]{:S(2)}) async-start(), calls=%async_computation.13 | async-start | bytes 4915200 | tf_op jit(solution)/shard_map/reduce_scatter | solution.py:174
  859.8 150.8 %reduce-scatter.21.cloned.1.call-start = ((), (), s32[]{:S(2)}) async-start(), calls=%async_computation.19 | async-start | bytes 2654208 | tf_op jit(solution)/shard_map/reduce_scatter | solution.py:216
  868.0 215.8 %reduce-scatter.23.cloned.1.call-start = ((), (), s32[]{:S(2)}) async-start(), calls=%async_computation.20 | async-start | bytes 2654208 | tf_op jit(solution)/shard_map/reduce_scatter | solution.py:217
  877.8 279.1 %reduce-scatter.19.cloned.1.call-start = ((), (), s32[]{:S(2)}) async-start(), calls=%async_computation.18 | async-start | bytes 2654208 | tf_op jit(solution)/shard_map/reduce_scatter | solution.py:214
  885.7 51.9 %copy-start.6 = (bf16[640,768]{1,0:T(8,128)(2,1)S(1)}, bf16[640,768]{1,0:T(8,128)(2,1)}, u32[]{:S(2)}) copy-start(bf16[640,768]{1,0:T(8,128)(2,1)} %reduce-scatter.11.cloned.1.call-done) | copy-start | bytes 2949124
  885.7 51.9 %copy-start.7 = (bf16[640,768]{1,0:T(8,128)(2,1)S(1)}, bf16[640,768]{1,0:T(8,128)(2,1)}, u32[]{:S(2)}) copy-start(bf16[640,768]{1,0:T(8,128)(2,1)} %param.16) | copy-start | bytes 2949124
  885.7 51.9 %copy-start.18 = (f32[640]{0:T(1024)S(1)}, f32[640]{0:T(1024)}, u32[]{:S(2)}) copy-start(f32[640]{0:T(1024)} %copy-done.17) | copy-start | bytes 7684
  885.7 51.9 %copy-start.22 = (f32[768]{0:T(1024)S(1)}, f32[768]{0:T(1024)}, u32[]{:S(2)}) copy-start(f32[768]{0:T(1024)} %copy-done.21) | copy-start | bytes 9220
  885.7 51.9 %copy-start.24 = (f32[640]{0:T(1024)S(1)}, f32[640]{0:T(1024)}, u32[]{:S(2)}) copy-start(f32[640]{0:T(1024)} %copy-done.23) | copy-start | bytes 7684
  885.7 51.9 %copy-start.31 = (f32[640]{0:T(1024)S(1)}, f32[640]{0:T(1024)}, u32[]{:S(2)}) copy-start(f32[640]{0:T(1024)} %copy-done.30) | copy-start | bytes 7684
  885.7 51.9 %copy-start.33 = (f32[640]{0:T(1024)S(1)}, f32[640]{0:T(1024)}, u32[]{:S(2)}) copy-start(f32[640]{0:T(1024)} %copy-done.32) | copy-start | bytes 7684
  (40 other events, 275.6 us)
Sparse Core Ops, SparseCore 0:
  43.1 30.2 all-gather.6
  247.1 42.4 reduce-scatter.10
  420.6 42.8 reduce-scatter.14
Sparse Core Ops, SparseCore 1:
  249.6 40.9 all-gather.12
  292.0 31.2 all-gather.14
  325.3 41.4 all-gather.10
  368.9 31.2 all-gather.8
  470.5 32.8 all-gather.16
  508.4 63.3 reduce-scatter.24
  848.7 42.8 reduce-scatter.16
  894.0 42.8 reduce-scatter.12
  940.8 69.8 reduce-scatter.20
  1014.7 69.0 reduce-scatter.22
  1087.7 69.1 reduce-scatter.18
where the time goes:
time: 1170 us; the launch traced here: 1160 us
  waiting for transfers between devices  433 us (37%)
  matrix products  348 us (30%)
  other arithmetic  148 us (13%)
  blocking collectives  137 us (12%)
  local copies, waits for them, and re-layouts  71.7 us (6%)
  between operations  17.7 us (2%)
    convert_element_type x5, other arithmetic, step(): score_grad = (prob * weight_grad - signed * inner).astype(jnp.bfloat16)  76.2 us
    dot_general x5, matrix products, step(): jnp.einsum('qhd,khd->hqk', grad_block, values, preferred_element_type=jnp...  75 us
    reduce_scatter x1, waiting for transfers between devices, on_device(): lax.psum_scatter(qkv_grad, 'dp', scatter_dimension=0, tiled=True)  73.1 us
    reduce_scatter x1, waiting for transfers between devices, on_device(): lax.psum_scatter(proj_grad, 'dp', scatter_dimension=1, tiled=True)  73.1 us
    dot_general x5, matrix products, step(): jnp.einsum('hqk,qhd->khd', rounded, grad_block, preferred_element_type=jn...  69.8 us
    reduce_scatter x1, waiting for transfers between devices, on_device(): lax.psum_scatter(fc_grad, 'dp', scatter_dimension=0, tiled=True)  68.8 us
    unnamed x2, blocking collectives  61 us
    dot_general x5, matrix products, one(): jnp.einsum('hqk,khd->qhd', weights, values, preferred_element_type=jnp.fl...  52.9 us
  transfers between devices with their start and end apart: 14, of which 10 were waited for; matrix products, arithmetic and copies ran while one was open for 34% of the time, Pallas kernels for 0%

commit v1 on v0

--- a/solution.py
+++ b/solution.py
@@ -5,6 +5,13 @@
 
 HEAD = 64
 PROMPT = 512
+
+
+def exchange_gather(x, name, dim):
+    size = lax.axis_size(name)
+    blocks = jnp.stack([x for _ in range(size)])
+    blocks = lax.all_to_all(blocks, name, split_axis=0, concat_axis=0)
+    return jnp.concatenate(blocks, axis=dim)
 
 
 def normalize(values):
@@ -166,7 +173,7 @@
     ).astype(jnp.float32)
     normed2, factor2 = normalize(resid)
     lowered2 = (normed2 * gain2 + bias2).astype(jnp.bfloat16)
-    all_norm2 = lax.all_gather(lowered2, "tensor", axis=0, tiled=True)
+    all_norm2 = exchange_gather(lowered2, "tensor", 0)
     hidden_pre = jnp.dot(all_norm2, fc_full, preferred_element_type=jnp.float32)
     hidden, gelu_pull = jax.vjp(gelu_tanh, hidden_pre)
     hidden_low = hidden.astype(jnp.bfloat16)

time: 1170 us -> 1150 us (0.983)
  waiting for transfers between devices: 433 us -> 411 us
    all_gather x1 -> x0, waiting for transfers between devices: 33.4 us -> none  [on_device(): all_norm2 = lax.all_gather(lowered2, 'tensor', axis=0, tiled=True)]
  transfers between devices with their start and end apart: 14 -> 14, of which waited for: 10 -> 9; matrix products, arithmetic and copies ran while one was open for 34% -> 34% of each run, Pallas kernels for 0% -> 0%
where the time goes in v1:
time: 1150 us
  waiting for transfers between devices  411 us (36%)
  matrix products  349 us (30%)
  other arithmetic  147 us (13%)
  blocking collectives  136 us (12%)
  local copies, waits for them, and re-layouts  73.6 us (6%)
  between operations  17.6 us (2%)
    convert_element_type x5, other arithmetic, step(): score_grad = (prob * weight_grad - signed * inner).astype(jnp.bfloat16)  76.2 us
    dot_general x5, matrix products, step(): jnp.einsum('qhd,khd->hqk', grad_block, values, preferred_element_type=jnp...  75.1 us
    reduce_scatter x1, waiting for transfers between devices, on_device(): lax.psum_scatter(qkv_grad, 'dp', scatter_dimension=0, tiled=True)  73.3 us
    reduce_scatter x1, waiting for transfers between devices, on_device(): lax.psum_scatter(proj_grad, 'dp', scatter_dimension=1, tiled=True)  72.9 us
    dot_general x5, matrix products, step(): jnp.einsum('hqk,qhd->khd', rounded, grad_block, preferred_element_type=jn...  69.8 us
    reduce_scatter x1, waiting for transfers between devices, on_device(): lax.psum_scatter(fc_grad, 'dp', scatter_dimension=0, tiled=True)  69.1 us
    unnamed x2, blocking collectives  61 us
    dot_general x5, matrix products, one(): jnp.einsum('hqk,khd->qhd', weights, values, preferred_element_type=jnp.fl...  52.9 us
  transfers between devices with their start and end apart: 14, of which 9 were waited for; matrix products, arithmetic and copies ran while one was open for 34% of the time, Pallas kernels for 0%

profile of v1, /device:TPU:0, one launch (start us, length us, event | category | flops | bytes accessed | tf_op | source)
XLA Modules:
  0.0 1148.1 jit_solution(13983338065964707319)
XLA Ops:
  13.4 23.9 %all-reduce.10 = (bf16[768]{0:T(1024)(128)(2,1)}, bf16[768]{0:T(1024)(128)(2,1)}, bf16[768]{0:T(1024)(128)(2,1)S(1)}, bf16[768]{0:T(1024)(128)(2,1)S(1)}) all-reduce(bf16[768]{0:T(1024)(128)(2,1)S(1)} %dynamic-update-slice.3, bf16[768]{0:T(1024)(128)(2,1)S(1)} %dynamic-update-slice.2, ...), channel_id=1, replica_groups=mesh['dp'=8,'tensor'=4] {'dp'}, use_global_device_ids=true, to_apply=%add.3 | all-reduce | flops 3072 | bytes 12288
  43.6 35.5 %all_gather.36 = bf16[768,3,192]{2,1,0:T(4,128)(2,1)S(1)} all-gather(bf16[96,3,192]{2,1,0:T(4,128)(2,1)S(1)} %copy.32), channel_id=1, replica_groups=mesh['dp'=8,'tensor'=4] {'dp'}, dimensions={0}, use_global_device_ids=true | all-gather | bytes 995328 | tf_op jit(solution)/shard_map/all_gather | solution.py:139
  80.1 33.4 %all_gather.37 = bf16[192,768]{0,1:T(8,128)(2,1)} all-gather(bf16[192,96]{0,1:T(8,128)(2,1)S(1)} %copy.35), channel_id=1, replica_groups=mesh['dp'=8,'tensor'=4] {'dp'}, dimensions={1}, use_global_device_ids=true | all-gather | bytes 331776 | tf_op jit(solution)/shard_map/all_gather | solution.py:140
  119.5 122.4 %while.29 = (s32[]{:T(128)}, bf16[5,512,3,64]{1,3,2,0:T(8,128)(2,1)S(1)}, f32[5,3,512]{2,1,0:T(4,128)S(1)}, s32[5]{0:T(128)S(1)}, bf16[2560,3,64]{0,2,1:T(8,128)...) while((s32[]{:T(128)}, ...), condition=%wide.region_7.8_spmd.clone, body=%wide.region_4.7_spmd.clone.sunk | while | flops 1086686208 | bytes 54895824 | solution.py:82
  157.7 10.6 fusion.127
  206.4 10.6 fusion.127
  248.4 41.4 %reduce-scatter.11.cloned.1.call-done = bf16[640,768]{1,0:T(8,128)(2,1)} async-done(((bf16[2560,768]{1,0:T(8,128)(2,1)}), bf16[640,768]{1,0:T(8,128)(2,1)}) %reduce-scatter.11.cloned.1.call-update) | async-done | bytes 983056 | tf_op jit(solution)/shard_map/reduce_scatter | solution.py:168
  301.3 40.3 %all-gather.12.cloned.1.call-done = bf16[2560,768]{1,0:T(8,128)(2,1)} async-done(((bf16[640,768]{1,0:T(8,128)(2,1)}), bf16[2560,768]{1,0:T(8,128)(2,1)}) %all-gather.12.cloned.1.call-update) | async-done | bytes 3932176 | tf_op jit(solution)/shard_map/all_gather | solution.py:188
  350.5 34.7 %all-gather.8.cloned.1.call-done = bf16[768,768]{1,0:T(8,128)(2,1)} async-done(((bf16[96,768]{1,0:T(8,128)(2,1)}), bf16[768,768]{1,0:T(8,128)(2,1)}) %all-gather.8.cloned.1.call-update) | async-done | bytes 1179664 | tf_op jit(solution)/shard_map/all_gather | solution.py:141
  385.2 13.8 %fusion.43 = (bf16[2560,768]{1,0:T(8,128)(2,1)S(1)}, f32[2560,768]{1,0:T(8,128)}) fusion(f32[2560,768]{1,0:T(8,128)} %fusion.75, bf16[2560,768]{1,0:T(8,128)(2,1)} %bitcast.8, bf16[768,768]{1,0:T(8,128)(2,1)} %all-gather.8.cloned.1.call-done), kind=kOutput, calls=%fused_computation.55 | convolution fusion | flops 3059220480 | bytes 24772608 | tf_op jit(solution)/shard_map/dot_general | solution.py:177
  405.8 41.2 %reduce-scatter.15.cloned.1.call-done = bf16[640,768]{1,0:T(8,128)(2,1)} async-done(((bf16[2560,768]{1,0:T(8,128)(2,1)}), bf16[640,768]{1,0:T(8,128)(2,1)}) %reduce-scatter.15.cloned.1.call-update) | async-done | bytes 983056 | tf_op jit(solution)/shard_map/reduce_scatter | solution.py:194
  453.9 33.1 %all-gather.14.cloned.1.call-done = bf16[2560,768]{1,0:T(8,128)(2,1)} async-done(((bf16[640,768]{1,0:T(8,128)(2,1)}), bf16[2560,768]{1,0:T(8,128)(2,1)}) %all-gather.14.cloned.1.call-update) | async-done | bytes 3932176 | tf_op jit(solution)/shard_map/all_gather | solution.py:201
  496.5 323.7 %while.30 = (s32[]{:T(128)}, f32[2560,3,64]{0,2,1:T(8,128)}, f32[2560,3,64]{0,2,1:T(8,128)}, bf16[5,512,3,64]{1,0,3,2:T(8,128)(2,1)}, s32[5]{0:T(128)S(1)}, /*in...) while((s32[]{:T(128)}, f32[2560,3,64]{0,2,1:T(8,128)}, ...), condition=%wide.region_17.18_spmd.clone.clone, body=%wide.region_15.17_spmd.clone.clone.sunk | while | flops 2622784512 | bytes 218457456 | solution.py:124
  503.3 12.2 %fusion.139 = f32[2560,3,64]{0,2,1:T(8,128)} fusion(f32[3,512,2560]{2,1,0:T(8,128)S(1)} %fusion.137, f32[3,512]{1,0:T(4,128)S(1)} %dynamic-slice_bitcast_fusion.2, pred[512,2560]{1,0:T(8,128)(4,1)S(1)} %or_and_fusion.5, f32[2560,3,64]{0,2,1:T(8,128)} %get-tuple-element.492, pred[]{:T(512)S(6)} %compare.3, ...), kind=kOutput, calls=%fused_computation.30.clone.1 | convolution fusion | flops 531824640 | bytes 21174276 | tf_op jit(solution)/shard_map/while/body/eval_jaxpr/hqk,qhd->khd/dot_general | solution.py:105
  515.5 15.0 %multiply_reduce_fusion.3 = (f32[3,512]{1,0:T(4,128)S(1)}, f32[3,512,2560]{2,1,0:T(8,128)}) fusion(f32[3,512,2560]{2,1,0:T(8,128)S(1)} %fusion.137, f32[3,512]{1,0:T(4,128)S(1)} %dynamic-slice_bitcast_fusion.2, pred[512,2560]{1,0:T(8,128)(4,1)S(1)} %or_and_fusion.5, bf16[2560,3,64]{0,2,1:T(8,128)(2,1)S(1)} %copy-done.12, ...), kind=kOutput, calls=%fused_computation.19.clone.1 | convolution fusion | flops 534772224 | bytes 33959940 | tf_op jit(solution)/shard_map/while/body/eval_jaxpr/qhd,khd->hqk/dot_general | solution.py:108
  530.6 15.2 %subtract_convert_fusion.2 = bf16[3,512,2560]{2,1,0:T(8,128)(2,1)S(1)} fusion(f32[3,512,2560]{2,1,0:T(8,128)} %get-tuple-element.433, f32[3,512,2560]{2,1,0:T(8,128)} %copy-done, f32[3,512]{1,0:T(4,128)S(1)} %get-tuple-element.434, f32[3,512]{1,0:T(4,128)S(1)} %dynamic-slice_bitcast_fusion.2, pred[512,2560]{1,0:T(8,128)(4,1)S(1)} %or_and_fusion.5), kind=kLoop, calls=%fused_computation.18.clone.1 | loop fusion | flops 39321600 | bytes 40644608 | tf_op jit(solution)/shard_map/while/body/eval_jaxpr/convert_element_type | solution.py:112
  566.2 14.4 %fusion.139 = f32[2560,3,64]{0,2,1:T(8,128)} fusion(f32[3,512,2560]{2,1,0:T(8,128)S(1)} %fusion.137, f32[3,512]{1,0:T(4,128)S(1)} %dynamic-slice_bitcast_fusion.2, pred[512,2560]{1,0:T(8,128)(4,1)S(1)} %or_and_fusion.5, f32[2560,3,64]{0,2,1:T(8,128)} %get-tuple-element.492, pred[]{:T(512)S(6)} %compare.3, ...), kind=kOutput, calls=%fused_computation.30.clone.1 | convolution fusion | flops 531824640 | bytes 21174276 | tf_op jit(solution)/shard_map/while/body/eval_jaxpr/hqk,qhd->khd/dot_general | solution.py:105
  580.6 15.0 %multiply_reduce_fusion.3 = (f32[3,512]{1,0:T(4,128)S(1)}, f32[3,512,2560]{2,1,0:T(8,128)}) fusion(f32[3,512,2560]{2,1,0:T(8,128)S(1)} %fusion.137, f32[3,512]{1,0:T(4,128)S(1)} %dynamic-slice_bitcast_fusion.2, pred[512,2560]{1,0:T(8,128)(4,1)S(1)} %or_and_fusion.5, bf16[2560,3,64]{0,2,1:T(8,128)(2,1)S(1)} %copy-done.12, ...), kind=kOutput, calls=%fused_computation.19.clone.1 | convolution fusion | flops 534772224 | bytes 33959940 | tf_op jit(solution)/shard_map/while/body/eval_jaxpr/qhd,khd->hqk/dot_general | solution.py:108
  595.7 15.2 %subtract_convert_fusion.2 = bf16[3,512,2560]{2,1,0:T(8,128)(2,1)S(1)} fusion(f32[3,512,2560]{2,1,0:T(8,128)} %get-tuple-element.433, f32[3,512,2560]{2,1,0:T(8,128)} %copy-done, f32[3,512]{1,0:T(4,128)S(1)} %get-tuple-element.434, f32[3,512]{1,0:T(4,128)S(1)} %dynamic-slice_bitcast_fusion.2, pred[512,2560]{1,0:T(8,128)(4,1)S(1)} %or_and_fusion.5), kind=kLoop, calls=%fused_computation.18.clone.1 | loop fusion | flops 39321600 | bytes 40644608 | tf_op jit(solution)/shard_map/while/body/eval_jaxpr/convert_element_type | solution.py:112
  631.3 14.4 %fusion.139 = f32[2560,3,64]{0,2,1:T(8,128)} fusion(f32[3,512,2560]{2,1,0:T(8,128)S(1)} %fusion.137, f32[3,512]{1,0:T(4,128)S(1)} %dynamic-slice_bitcast_fusion.2, pred[512,2560]{1,0:T(8,128)(4,1)S(1)} %or_and_fusion.5, f32[2560,3,64]{0,2,1:T(8,128)} %get-tuple-element.492, pred[]{:T(512)S(6)} %compare.3, ...), kind=kOutput, calls=%fused_computation.30.clone.1 | convolution fusion | flops 531824640 | bytes 21174276 | tf_op jit(solution)/shard_map/while/body/eval_jaxpr/hqk,qhd->khd/dot_general | solution.py:105
  645.7 15.0 %multiply_reduce_fusion.3 = (f32[3,512]{1,0:T(4,128)S(1)}, f32[3,512,2560]{2,1,0:T(8,128)}) fusion(f32[3,512,2560]{2,1,0:T(8,128)S(1)} %fusion.137, f32[3,512]{1,0:T(4,128)S(1)} %dynamic-slice_bitcast_fusion.2, pred[512,2560]{1,0:T(8,128)(4,1)S(1)} %or_and_fusion.5, bf16[2560,3,64]{0,2,1:T(8,128)(2,1)S(1)} %copy-done.12, ...), kind=kOutput, calls=%fused_computation.19.clone.1 | convolution fusion | flops 534772224 | bytes 33959940 | tf_op jit(solution)/shard_map/while/body/eval_jaxpr/qhd,khd->hqk/dot_general | solution.py:108
  660.7 15.2 %subtract_convert_fusion.2 = bf16[3,512,2560]{2,1,0:T(8,128)(2,1)S(1)} fusion(f32[3,512,2560]{2,1,0:T(8,128)} %get-tuple-element.433, f32[3,512,2560]{2,1,0:T(8,128)} %copy-done, f32[3,512]{1,0:T(4,128)S(1)} %get-tuple-element.434, f32[3,512]{1,0:T(4,128)S(1)} %dynamic-slice_bitcast_fusion.2, pred[512,2560]{1,0:T(8,128)(4,1)S(1)} %or_and_fusion.5), kind=kLoop, calls=%fused_computation.18.clone.1 | loop fusion | flops 39321600 | bytes 40644608 | tf_op jit(solution)/shard_map/while/body/eval_jaxpr/convert_element_type | solution.py:112
  696.4 14.4 %fusion.139 = f32[2560,3,64]{0,2,1:T(8,128)} fusion(f32[3,512,2560]{2,1,0:T(8,128)S(1)} %fusion.137, f32[3,512]{1,0:T(4,128)S(1)} %dynamic-slice_bitcast_fusion.2, pred[512,2560]{1,0:T(8,128)(4,1)S(1)} %or_and_fusion.5, f32[2560,3,64]{0,2,1:T(8,128)} %get-tuple-element.492, pred[]{:T(512)S(6)} %compare.3, ...), kind=kOutput, calls=%fused_computation.30.clone.1 | convolution fusion | flops 531824640 | bytes 21174276 | tf_op jit(solution)/shard_map/while/body/eval_jaxpr/hqk,qhd->khd/dot_general | solution.py:105
  710.8 15.0 %multiply_reduce_fusion.3 = (f32[3,512]{1,0:T(4,128)S(1)}, f32[3,512,2560]{2,1,0:T(8,128)}) fusion(f32[3,512,2560]{2,1,0:T(8,128)S(1)} %fusion.137, f32[3,512]{1,0:T(4,128)S(1)} %dynamic-slice_bitcast_fusion.2, pred[512,2560]{1,0:T(8,128)(4,1)S(1)} %or_and_fusion.5, bf16[2560,3,64]{0,2,1:T(8,128)(2,1)S(1)} %copy-done.12, ...), kind=kOutput, calls=%fused_computation.19.clone.1 | convolution fusion | flops 534772224 | bytes 33959940 | tf_op jit(solution)/shard_map/while/body/eval_jaxpr/qhd,khd->hqk/dot_general | solution.py:108
  725.8 15.2 %subtract_convert_fusion.2 = bf16[3,512,2560]{2,1,0:T(8,128)(2,1)S(1)} fusion(f32[3,512,2560]{2,1,0:T(8,128)} %get-tuple-element.433, f32[3,512,2560]{2,1,0:T(8,128)} %copy-done, f32[3,512]{1,0:T(4,128)S(1)} %get-tuple-element.434, f32[3,512]{1,0:T(4,128)S(1)} %dynamic-slice_bitcast_fusion.2, pred[512,2560]{1,0:T(8,128)(4,1)S(1)} %or_and_fusion.5), kind=kLoop, calls=%fused_computation.18.clone.1 | loop fusion | flops 39321600 | bytes 40644608 | tf_op jit(solution)/shard_map/while/body/eval_jaxpr/convert_element_type | solution.py:112
  761.4 14.4 %fusion.139 = f32[2560,3,64]{0,2,1:T(8,128)} fusion(f32[3,512,2560]{2,1,0:T(8,128)S(1)} %fusion.137, f32[3,512]{1,0:T(4,128)S(1)} %dynamic-slice_bitcast_fusion.2, pred[512,2560]{1,0:T(8,128)(4,1)S(1)} %or_and_fusion.5, f32[2560,3,64]{0,2,1:T(8,128)} %get-tuple-element.492, pred[]{:T(512)S(6)} %compare.3, ...), kind=kOutput, calls=%fused_computation.30.clone.1 | convolution fusion | flops 531824640 | bytes 21174276 | tf_op jit(solution)/shard_map/while/body/eval_jaxpr/hqk,qhd->khd/dot_general | solution.py:105
  775.8 15.0 %multiply_reduce_fusion.3 = (f32[3,512]{1,0:T(4,128)S(1)}, f32[3,512,2560]{2,1,0:T(8,128)}) fusion(f32[3,512,2560]{2,1,0:T(8,128)S(1)} %fusion.137, f32[3,512]{1,0:T(4,128)S(1)} %dynamic-slice_bitcast_fusion.2, pred[512,2560]{1,0:T(8,128)(4,1)S(1)} %or_and_fusion.5, bf16[2560,3,64]{0,2,1:T(8,128)(2,1)S(1)} %copy-done.12, ...), kind=kOutput, calls=%fused_computation.19.clone.1 | convolution fusion | flops 534772224 | bytes 33959940 | tf_op jit(solution)/shard_map/while/body/eval_jaxpr/qhd,khd->hqk/dot_general | solution.py:108
  790.9 15.2 %subtract_convert_fusion.2 = bf16[3,512,2560]{2,1,0:T(8,128)(2,1)S(1)} fusion(f32[3,512,2560]{2,1,0:T(8,128)} %get-tuple-element.433, f32[3,512,2560]{2,1,0:T(8,128)} %copy-done, f32[3,512]{1,0:T(4,128)S(1)} %get-tuple-element.434, f32[3,512]{1,0:T(4,128)S(1)} %dynamic-slice_bitcast_fusion.2, pred[512,2560]{1,0:T(8,128)(4,1)S(1)} %or_and_fusion.5), kind=kLoop, calls=%fused_computation.18.clone.1 | loop fusion | flops 39321600 | bytes 40644608 | tf_op jit(solution)/shard_map/while/body/eval_jaxpr/convert_element_type | solution.py:112
  877.4 37.1 %all-reduce.8 = (f32[768]{0:T(1024)S(1)}, f32[768]{0:T(1024)S(1)}, f32[768]{0:T(1024)S(1)}, f32[768]{0:T(1024)S(1)}) all-reduce(f32[768]{0:T(1024)S(1)} %get-tuple-element.224, f32[768]{0:T(1024)S(1)} %get-tuple-element.229, f32[768]{0:T(1024)S(1)} %copy-done.34, ...), channel_id=10, replica_groups=mesh['dp'=8,'tensor'=4] {'dp'}, use_global_device_ids=true, to_apply=%region_26.27.clone | all-reduce | flops 3072 | bytes 24576
  925.4 69.1 %reduce-scatter.21.cloned.1.call-done = f32[96,768]{1,0:T(8,128)} async-done(((f32[768,768]{1,0:T(8,128)}), f32[96,768]{1,0:T(8,128)}) %reduce-scatter.21.cloned.1.call-update) | async-done | bytes 294928 | tf_op jit(solution)/shard_map/reduce_scatter | solution.py:223
  994.5 72.9 %reduce-scatter.23.cloned.1.call-done = f32[768,96]{0,1:T(8,128)} async-done(((f32[768,768]{0,1:T(8,128)}), f32[768,96]{0,1:T(8,128)}) %reduce-scatter.23.cloned.1.call-update) | async-done | bytes 294928 | tf_op jit(solution)/shard_map/reduce_scatter | solution.py:224
  1067.4 73.3 %reduce-scatter.19.cloned.1.call-done = f32[96,3,192]{2,0,1:T(8,128)} async-done(((f32[768,3,192]{2,0,1:T(8,128)}), f32[96,3,192]{2,0,1:T(8,128)}) %reduce-scatter.19.cloned.1.call-update) | async-done | bytes 221200 | tf_op jit(solution)/shard_map/reduce_scatter | solution.py:221
  (316 shorter events, 330.1 us)
Async XLA Ops:
  8.0 35.1 %copy-start.40 = (s32[1,8]{1,0:T(1,128)S(1)}, s32[1,8]{1,0:T(1,128)}, u32[]{:S(2)}) copy-start(s32[1,8]{1,0:T(1,128)} %param.17) | copy-start | bytes 100
  8.0 35.3 %copy-start.29 = (bf16[192,96]{1,0:T(8,128)(2,1)S(1)}, bf16[192,96]{1,0:T(8,128)(2,1)}, u32[]{:S(2)}) copy-start(bf16[192,96]{1,0:T(8,128)(2,1)} %param.19) | copy-start | bytes 110596
  8.0 35.4 %copy-start.16 = (bf16[96,3,192]{2,0,1:T(8,128)(2,1)S(1)}, bf16[96,3,192]{2,0,1:T(8,128)(2,1)}, u32[]{:S(2)}) copy-start(bf16[96,3,192]{2,0,1:T(8,128)(2,1)} %param.18) | copy-start | bytes 331780
  8.0 105.5 %all-gather.6.cloned.1.call-start = ((), (), s32[]{:S(2)}) async-start(), calls=%async_computation.9 | async-start | bytes 4915200 | tf_op jit(solution)/shard_map/all_gather | solution.py:160
  43.0 246.8 %reduce-scatter.11.cloned.1.call-start = ((), (), s32[]{:S(2)}) async-start(), calls=%async_computation.10 | async-start | bytes 4915200 | tf_op jit(solution)/shard_map/reduce_scatter | solution.py:168
  80.0 38.2 %copy-start.14 = (bf16[768,3,192]{0,2,1:T(8,128)(2,1)}, bf16[768,3,192]{0,2,1:T(8,128)(2,1)S(1)}, u32[]{:S(2)}) copy-start(bf16[768,3,192]{0,2,1:T(8,128)(2,1)S(1)} %copy.33) | copy-start | bytes 2654212
  247.1 42.7 %copy-start.1 = (bf16[640,768]{1,0:T(8,128)(2,1)S(1)}, bf16[640,768]{1,0:T(8,128)(2,1)}, u32[]{:S(2)}) copy-start(bf16[640,768]{1,0:T(8,128)(2,1)} %param.15) | copy-start | bytes 2949124
  247.1 54.2 %all-gather.10.cloned.1.call-start = ((), (), s32[]{:S(2)}) async-start(), calls=%async_computation.12 | async-start | bytes 1327104 | tf_op jit(solution)/shard_map/all_gather | solution.py:142
  247.7 94.0 %all-gather.12.cloned.1.call-start = ((), (), s32[]{:S(2)}) async-start(), calls=%async_computation.14 | async-start | bytes 4915200 | tf_op jit(solution)/shard_map/all_gather | solution.py:188
  248.3 201.5 %copy-start.21 = (f32[768]{0:T(1024)}, f32[768]{0:T(1024)S(1)}, u32[]{:S(2)}) copy-start(f32[768]{0:T(1024)S(1)} %convert_element_type.109) | copy-start | bytes 9220
  291.4 158.4 %copy-start.17 = (f32[640]{0:T(1024)}, f32[640]{0:T(1024)S(1)}, u32[]{:S(2)}) copy-start(f32[640]{0:T(1024)S(1)} %broadcast_multiply_fusion.4) | copy-start | bytes 7684
  293.1 156.7 %copy-start.23 = (f32[640]{0:T(1024)}, f32[640]{0:T(1024)S(1)}, u32[]{:S(2)}) copy-start(f32[640]{0:T(1024)S(1)} %add_rsqrt_fusion) | copy-start | bytes 7684
  295.8 89.4 %all-to-all-start = ((bf16[4,640,768]{2,1,0:T(8,128)(2,1)}), bf16[4,640,768]{2,1,0:T(8,128)(2,1)}, u32[]{:S(2)}, u32[]{:S(2)}) async-start(bf16[4,640,768]{2,1,0:T(8,128)(2,1)} %stack.16), calls=%async_computation.1 | async-start | bytes 7864320 | tf_op jit(solution)/shard_map/all_to_all | solution.py:13
  300.7 84.5 %all-gather.8.cloned.1.call-start = ((), (), s32[]{:S(2)}) async-start(), calls=%async_computation.11 | async-start | bytes 1327104 | tf_op jit(solution)/shard_map/all_gather | solution.py:141
  301.3 145.7 %reduce-scatter.15.cloned.1.call-start = ((), (), s32[]{:S(2)}) async-start(), calls=%async_computation.15 | async-start | bytes 4915200 | tf_op jit(solution)/shard_map/reduce_scatter | solution.py:194
  385.2 15.8 %copy-start.39 = (bf16[768,768]{1,0:T(8,128)(2,1)S(1)}, bf16[768,768]{1,0:T(8,128)(2,1)}, u32[]{:S(2)}) copy-start(bf16[768,768]{1,0:T(8,128)(2,1)} %all-gather.8.cloned.1.call-done) | copy-start | bytes 3538948
  405.7 81.2 %all-gather.14.cloned.1.call-start = ((), (), s32[]{:S(2)}) async-start(), calls=%async_computation.16 | async-start | bytes 4915200 | tf_op jit(solution)/shard_map/all_gather | solution.py:201
  453.8 416.4 %reduce-scatter.25.cloned.1.call-start = ((), (), s32[]{:S(2)}) async-start(), calls=%async_computation.21 | async-start | bytes 884736
  491.9 383.2 %reduce-scatter.17.cloned.1.call-start = ((), (), s32[]{:S(2)}) async-start(), calls=%async_computation.17 | async-start | bytes 4915200 | tf_op jit(solution)/shard_map/reduce_scatter | solution.py:214
  631.3 14.4 %copy-start = (f32[3,512,2560]{2,1,0:T(8,128)}, f32[3,512,2560]{2,1,0:T(8,128)S(1)}, u32[]{:S(2)}) copy-start(f32[3,512,2560]{2,1,0:T(8,128)S(1)} %fusion.137) | copy-start | bytes 47185924 | tf_op jit(solution)/shard_map/while
  696.3 14.4 %copy-start = (f32[3,512,2560]{2,1,0:T(8,128)}, f32[3,512,2560]{2,1,0:T(8,128)S(1)}, u32[]{:S(2)}) copy-start(f32[3,512,2560]{2,1,0:T(8,128)S(1)} %fusion.137) | copy-start | bytes 47185924 | tf_op jit(solution)/shard_map/while
  832.3 88.9 %reduce-scatter.13.cloned.1.call-start = ((), (), s32[]{:S(2)}) async-start(), calls=%async_computation.13 | async-start | bytes 4915200 | tf_op jit(solution)/shard_map/reduce_scatter | solution.py:181
  843.4 151.1 %reduce-scatter.21.cloned.1.call-start = ((), (), s32[]{:S(2)}) async-start(), calls=%async_computation.19 | async-start | bytes 2654208 | tf_op jit(solution)/shard_map/reduce_scatter | solution.py:223
  851.6 215.9 %reduce-scatter.23.cloned.1.call-start = ((), (), s32[]{:S(2)}) async-start(), calls=%async_computation.20 | async-start | bytes 2654208 | tf_op jit(solution)/shard_map/reduce_scatter | solution.py:224
  861.5 279.2 %reduce-scatter.19.cloned.1.call-start = ((), (), s32[]{:S(2)}) async-start(), calls=%async_computation.18 | async-start | bytes 2654208 | tf_op jit(solution)/shard_map/reduce_scatter | solution.py:221
  869.3 51.9 %copy-start.6 = (bf16[640,768]{1,0:T(8,128)(2,1)S(1)}, bf16[640,768]{1,0:T(8,128)(2,1)}, u32[]{:S(2)}) copy-start(bf16[640,768]{1,0:T(8,128)(2,1)} %reduce-scatter.11.cloned.1.call-done) | copy-start | bytes 2949124
  869.3 51.9 %copy-start.7 = (bf16[640,768]{1,0:T(8,128)(2,1)S(1)}, bf16[640,768]{1,0:T(8,128)(2,1)}, u32[]{:S(2)}) copy-start(bf16[640,768]{1,0:T(8,128)(2,1)} %param.16) | copy-start | bytes 2949124
  869.3 51.9 %copy-start.18 = (f32[640]{0:T(1024)S(1)}, f32[640]{0:T(1024)}, u32[]{:S(2)}) copy-start(f32[640]{0:T(1024)} %copy-done.17) | copy-start | bytes 7684
  869.3 51.9 %copy-start.22 = (f32[768]{0:T(1024)S(1)}, f32[768]{0:T(1024)}, u32[]{:S(2)}) copy-start(f32[768]{0:T(1024)} %copy-done.21) | copy-start | bytes 9220
  869.3 51.9 %copy-start.24 = (f32[640]{0:T(1024)S(1)}, f32[640]{0:T(1024)}, u32[]{:S(2)}) copy-start(f32[640]{0:T(1024)} %copy-done.23) | copy-start | bytes 7684
  869.4 51.9 %copy-start.31 = (f32[640]{0:T(1024)S(1)}, f32[640]{0:T(1024)}, u32[]{:S(2)}) copy-start(f32[640]{0:T(1024)} %copy-done.30) | copy-start | bytes 7684
  869.4 51.9 %copy-start.33 = (f32[640]{0:T(1024)S(1)}, f32[640]{0:T(1024)}, u32[]{:S(2)}) copy-start(f32[640]{0:T(1024)} %copy-done.32) | copy-start | bytes 7684
  (40 other events, 273.8 us)
Sparse Core Ops, SparseCore 0:
  43.1 30.2 all-gather.5
  247.3 42.4 reduce-scatter.10
  453.9 32.9 all-gather.13
Sparse Core Ops, SparseCore 1:
  249.8 41.0 all-gather.9
  292.3 49.4 all-gather.11
  343.7 41.4 all-gather.7
  405.8 41.1 reduce-scatter.14
  492.0 63.3 reduce-scatter.24
  832.3 42.8 reduce-scatter.16
  877.6 42.8 reduce-scatter.12
  924.3 70.1 reduce-scatter.20
  998.4 68.9 reduce-scatter.22
  1071.5 69.1 reduce-scatter.18
